TPU v7x, 32 devices: a whole 2x2x4 slice. The times are simulated.
32 devices in a mesh: samp: 16 (over z, y, x), feat: 2 (over core).
Axes of the slice: x: 2, y: 2, z: 4, core: 2. Of those that a mesh axis runs over, the one named last changes fastest.
Arguments:
- design_matrix: bfloat16 [2048, 32768], P('samp', 'feat'), may hold values from -0.046875 to 0.046875
- labels: int32 [2048], P('samp'), may hold values from 0 to 1
- weights: float32 [16, 32768], P(None, ('feat', 'samp')), may hold values from -6 to 6
- lambdas: float32 [16], replicated, may hold values from 0.05 to 1
- sketch: bfloat16 [32768, 384], P(('feat', 'samp')), may hold values from -0.03125 to 0.03125
- sketch_values: float32 [384], replicated, may hold values from 0.05 to 2
Outputs:
- new_weights: float32 [16, 32768], P(None, ('feat', 'samp'))
All inputs are finite; a program needn't handle non-finite values.
Results may differ from a plain program's by a relative error of at most 0.004.
Values may be sent and summed in bfloat16 or wider, within the bound.
No kernel may reach another device: no remote copies, remote signals or barrier semaphores. Data moves between devices by JAX's collectives and lax.ppermute only.
A program may use at most 64 MiB of HBM per device.

v0:
```python
import jax
import jax.numpy as jnp
from jax import lax
from jax.sharding import PartitionSpec as P

ITERS = 2


def shards(design_matrix, labels, weights, lambdas, sketch, sketch_values):
    sketch_full = sketch.astype(jnp.float32)
    smallest = jnp.min(sketch_values)
    ratios = (smallest + lambdas[:, None]) / (sketch_values[None, :] + lambdas[:, None]) - 1.0

    def apply_rows(vector):
        vector_half = vector.astype(jnp.bfloat16)
        partial_rows = lax.dot_general(
            lax.all_gather(vector_half, "samp", axis=1, tiled=True),
            design_matrix,
            (((1,), (1,)), ((), ())),
            preferred_element_type=jnp.float32,
        )
        return lax.psum(partial_rows, "feat")

    def apply_columns(values):
        return lax.psum_scatter(
            lax.dot_general(
                design_matrix, values, (((0,), (1,)), ((), ())), preferred_element_type=jnp.float32
            ),
            "samp",
            scatter_dimension=0,
            tiled=True,
        ).T

    def precondition(residual):
        projected = jnp.dot(residual, sketch_full, precision=lax.Precision.HIGHEST)
        projected = lax.psum(projected, ("samp", "feat"))
        correction = lax.dot_general(
            ratios * projected,
            sketch_full,
            (((1,), (1,)), ((), ())),
            precision=lax.Precision.HIGHEST,
        )
        precond_res = residual + correction
        res_dot = lax.psum(jnp.sum(residual * precond_res, axis=1), ("samp", "feat"))
        return (precond_res, res_dot)

    logits = apply_rows(weights)
    probability = jax.nn.sigmoid(logits)
    hessian_diag = probability * (1.0 - probability)
    miss_rows = (probability - labels[None, :].astype(jnp.float32)).astype(jnp.bfloat16)
    gradient = apply_columns(miss_rows) + lambdas[:, None] * weights
    residual = -gradient
    precond_res, res_dot = precondition(residual)
    direction = precond_res
    update = jnp.zeros_like(residual)
    for iteration in range(ITERS):
        image_rows = apply_rows(direction)
        hess_dir = (
            apply_columns((hessian_diag * image_rows).astype(jnp.bfloat16))
            + lambdas[:, None] * direction
        )
        curvature = lax.psum(jnp.sum(direction * hess_dir, axis=1), ("samp", "feat"))
        step_size = res_dot / curvature
        update = update + step_size[:, None] * direction
        if iteration + 1 < ITERS:
            residual = residual - step_size[:, None] * hess_dir
            precond_res, new_dot = precondition(residual)
            direction = precond_res + (new_dot / res_dot)[:, None] * direction
            res_dot = new_dot
    return weights + update


def solution(mesh):
    return jax.shard_map(
        shards,
        mesh=mesh,
        in_specs=(
            P("samp", "feat"),
            P("samp"),
            P(None, ("feat", "samp")),
            P(),
            P(("feat", "samp"), None),
            P(),
        ),
        out_specs=P(None, ("feat", "samp")),
        check_vma=False,
    )
```

profile of v0, /device:TPU:10, one launch (start us, length us, event | category | flops | bytes accessed | tf_op | source)
XLA Modules:
  0.0 596.1 jit_solution(18189731865618623638)
XLA Ops:
  8.1 33.0 %all_gather.9 = bf16[16,16384]{1,0:T(8,128)(2,1)S(1)} all-gather(bf16[16,1024]{1,0:T(8,128)(2,1)S(1)} %convert_element_type.23), channel_id=1, replica_groups=mesh['samp'=16,'feat'=2] {'samp'}, dimensions={1}, use_global_device_ids=true | all-gather | bytes 557056 | tf_op jit(solution)/shard_map/all_gather | solution.py:17
  41.1 3.4 fusion.22
  44.5 2.6 psum.63
  47.1 3.8 convolution_bitcast_fusion.2
  52.3 73.3 %reduce-scatter.4.cloned.1.call-done = f32[1024,16]{0,1:T(8,128)} async-done(((f32[16384,16]{0,1:T(8,128)}), f32[1024,16]{0,1:T(8,128)}) %reduce-scatter.4.cloned.1.call-update) | async-done | bytes 65552 | tf_op jit(solution)/shard_map/reduce_scatter | solution.py:25
  125.6 0.9 fusion.2
  127.0 50.1 %psum.64 = f32[16,384]{1,0:T(8,128)S(1)} all-reduce(f32[16,384]{1,0:T(8,128)S(1)} %fusion.23), channel_id=1, replica_groups=mesh['samp'=16,'feat'=2] {'samp','feat'}, use_global_device_ids=true, to_apply=%region_3.0 | all-reduce | flops 6144 | bytes 49152 | tf_op jit(solution)/shard_map/psum | solution.py:36
  177.8 32.0 %all_gather.10 = bf16[16,16384]{1,0:T(8,128)(2,1)S(1)} all-gather(bf16[16,1024]{1,0:T(8,128)(2,1)S(1)} %get-tuple-element.9), channel_id=1, replica_groups=mesh['samp'=16,'feat'=2] {'samp'}, dimensions={1}, use_global_device_ids=true | all-gather | bytes 557056 | tf_op jit(solution)/shard_map/all_gather | solution.py:17
  209.8 3.4 fusion.24
  213.1 2.5 psum.66
  215.6 3.8 convolution_bitcast_fusion.1
  219.5 71.6 %reduce-scatter.6.cloned.1.call-done = f32[1024,16]{0,1:T(8,128)} async-done(((f32[16384,16]{0,1:T(8,128)}), f32[1024,16]{0,1:T(8,128)}) %reduce-scatter.6.cloned.1.call-update) | async-done | bytes 65552 | tf_op jit(solution)/shard_map/reduce_scatter | solution.py:25
  291.1 1.0 multiply_reduce_fusion.1
  292.1 49.7 %all-reduce = (f32[16]{0:T(128)S(1)}, f32[16]{0:T(128)S(1)}) all-reduce(f32[16]{0:T(128)S(1)} %get-tuple-element.6, f32[16]{0:T(128)S(1)} %get-tuple-element.5), channel_id=1, replica_groups=mesh['samp'=16,'feat'=2] {'samp','feat'}, use_global_device_ids=true, to_apply=%region_5.0 | all-reduce | flops 32 | bytes 256 | tf_op jit(solution)/shard_map/psum | solution.py:44
  341.9 0.9 multiply_subtract_fusion
  343.2 38.3 %psum.68 = f32[16,384]{1,0:T(8,128)S(1)} all-reduce(f32[16,384]{1,0:T(8,128)S(1)} %fusion.25), channel_id=1, replica_groups=mesh['samp'=16,'feat'=2] {'samp','feat'}, use_global_device_ids=true, to_apply=%region_10.0 | all-reduce | flops 6144 | bytes 49152 | tf_op jit(solution)/shard_map/psum | solution.py:36
  382.3 41.9 %psum.69 = f32[16]{0:T(128)S(1)} all-reduce(f32[16]{0:T(128)S(1)} %get-tuple-element.11), channel_id=1, replica_groups=mesh['samp'=16,'feat'=2] {'samp','feat'}, use_global_device_ids=true, to_apply=%region_12.0 | all-reduce | flops 16 | bytes 128 | tf_op jit(solution)/shard_map/psum | solution.py:44
  424.3 31.8 %all_gather.11 = bf16[16,16384]{1,0:T(8,128)(2,1)S(1)} all-gather(bf16[16,1024]{1,0:T(8,128)(2,1)S(1)} %fusion.20), channel_id=1, replica_groups=mesh['samp'=16,'feat'=2] {'samp'}, dimensions={1}, use_global_device_ids=true | all-gather | bytes 557056 | tf_op jit(solution)/shard_map/all_gather | solution.py:17
  456.1 3.4 fusion.26
  459.5 2.5 psum.70
  462.0 3.9 convolution_bitcast_fusion
  465.8 72.2 %reduce-scatter.8.cloned.1.call-done = f32[1024,16]{0,1:T(8,128)} async-done(((f32[16384,16]{0,1:T(8,128)}), f32[1024,16]{0,1:T(8,128)}) %reduce-scatter.8.cloned.1.call-update) | async-done | bytes 65552 | tf_op jit(solution)/shard_map/reduce_scatter | solution.py:25
  538.1 1.0 fusion.1
  539.1 49.8 %psum.71 = f32[16]{0:T(128)S(1)} all-reduce(f32[16]{0:T(128)S(1)} %fusion.1), channel_id=1, replica_groups=mesh['samp'=16,'feat'=2] {'samp','feat'}, use_global_device_ids=true, to_apply=%region_16.0 | all-reduce | flops 16 | bytes 128 | tf_op jit(solution)/shard_map/psum | solution.py:62
  (27 shorter events, 6.2 us)
Async XLA Ops:
  6.5 120.0 %copy-start = (bf16[1024,384]{1,0:T(8,128)(2,1)S(1)}, bf16[1024,384]{1,0:T(8,128)(2,1)}, u32[]{:S(2)}) copy-start(bf16[1024,384]{1,0:T(8,128)(2,1)} %param.10) | copy-start | bytes 2359300
  6.5 119.1 %reduce-scatter.4.cloned.1.call-start = ((), (), s32[]{:S(2)}) async-start(), calls=%async_computation.3 | async-start | bytes 1114112 | tf_op jit(solution)/shard_map/reduce_scatter | solution.py:25
  44.4 6.6 %copy-start.3 = (f32[384]{0:T(512)S(1)}, f32[384]{0:T(512)}, u32[]{:S(2)}) copy-start(f32[384]{0:T(512)} %param.11) | copy-start | bytes 4612
  44.4 7.2 %copy-start.2 = (f32[16]{0:T(128)S(1)}, f32[16]{0:T(128)}, u32[]{:S(2)}) copy-start(f32[16]{0:T(128)} %param.9) | copy-start | bytes 196
  44.4 81.2 %copy-start.1 = (f32[16,1024]{1,0:T(8,128)S(1)}, f32[16,1024]{1,0:T(8,128)}, u32[]{:S(2)}) copy-start(f32[16,1024]{1,0:T(8,128)} %param.8) | copy-start | bytes 196612
  51.0 240.1 %reduce-scatter.6.cloned.1.call-start = ((), (), s32[]{:S(2)}) async-start(), calls=%async_computation.4 | async-start | bytes 1114112 | tf_op jit(solution)/shard_map/reduce_scatter | solution.py:25
  219.5 318.6 %reduce-scatter.8.cloned.1.call-start = ((), (), s32[]{:S(2)}) async-start(), calls=%async_computation.5 | async-start | bytes 1114112 | tf_op jit(solution)/shard_map/reduce_scatter | solution.py:25
Sparse Core Ops, SparseCore 0:
  51.1 74.4 reduce-scatter.3
  219.6 71.4 reduce-scatter.5
  466.0 72.0 reduce-scatter.7
where the time goes:
time: 597 us; the launch traced here: 596 us
  blocking collectives  334 us (56%)
  waiting for transfers between devices  217 us (36%)
  matrix products  24.1 us (4%)
  between operations  13.2 us (2%)
  other arithmetic  7.54 us (1%)
    reduce_scatter x3, waiting for transfers between devices, apply_columns(): lax.psum_scatter(lax.dot_general(design_matrix, values, (((0,), (1,)), ((...  217 us
    all_gather x3, blocking collectives, apply_rows(): lax.all_gather(vector_half, 'samp', axis=1, tiled=True)  96.7 us
    psum x2, blocking collectives, precondition(): lax.psum(jnp.sum(residual * precond_res, axis=1), ('samp', 'feat'))  91.6 us
    psum x2, blocking collectives, precondition(): projected = lax.psum(projected, ('samp', 'feat'))  88.3 us
    psum x1, blocking collectives, shards(): lax.psum(jnp.sum(direction * hess_dir, axis=1), ('samp', 'feat'))  49.8 us
  transfers between devices with their start and end apart: 3, of which 3 were waited for; matrix products, arithmetic and copies ran while one was open for 0% of the time, Pallas kernels for 0%

commit v1 on v0

--- a/solution.py
+++ b/solution.py
@@ -59,7 +59,7 @@
             apply_columns((hessian_diag * image_rows).astype(jnp.bfloat16))
             + lambdas[:, None] * direction
         )
-        curvature = lax.psum(jnp.sum(direction * hess_dir, axis=1), ("samp", "feat"))
+        curvature = lax.psum(lax.psum(jnp.sum(direction * hess_dir, axis=1), "feat"), "samp")
         step_size = res_dot / curvature
         update = update + step_size[:, None] * direction
         if iteration + 1 < ITERS:

time: 597 us -> 640 us (1.072); the launches traced: 596 us -> 631 us
  blocking collectives: 334 us -> 368 us
    psum x1 -> x4, blocking collectives: 49.8 us -> 88.1 us  [the longest x2 83.2 us: shards(): lax.psum(lax.psum(jnp.sum(direction * hess_dir, axis=1), 'feat'), 'samp')]
where the time goes in v1:
time: 640 us; the launch traced here: 631 us
  blocking collectives  368 us (58%)
  waiting for transfers between devices  218 us (34%)
  matrix products  24.1 us (4%)
  between operations  13.2 us (2%)
  other arithmetic  7.54 us (1%)
    reduce_scatter x3, waiting for transfers between devices, apply_columns(): lax.psum_scatter(lax.dot_general(design_matrix, values, (((0,), (1,)), ((...  218 us
    all_gather x3, blocking collectives, apply_rows(): lax.all_gather(vector_half, 'samp', axis=1, tiled=True)  96.5 us
    psum x2, blocking collectives, precondition(): projected = lax.psum(projected, ('samp', 'feat'))  89.5 us
    psum x2, blocking collectives, precondition(): lax.psum(jnp.sum(residual * precond_res, axis=1), ('samp', 'feat'))  86.1 us
    psum x2, blocking collectives, shards(): lax.psum(lax.psum(jnp.sum(direction * hess_dir, axis=1), 'feat'), 'samp')  83.2 us
  transfers between devices with their start and end apart: 3, of which 3 were waited for; matrix products, arithmetic and copies ran while one was open for 0% of the time, Pallas kernels for 0%

profile of v1, /device:TPU:10, one launch (start us, length us, event | category | flops | bytes accessed | tf_op | source)
XLA Modules:
  0.0 631.0 jit_solution(8417049769428493381)
XLA Ops:
  8.1 33.0 %all_gather.9 = bf16[16,16384]{1,0:T(8,128)(2,1)S(1)} all-gather(bf16[16,1024]{1,0:T(8,128)(2,1)S(1)} %convert_element_type.23), channel_id=1, replica_groups=mesh['samp'=16,'feat'=2] {'samp'}, dimensions={1}, use_global_device_ids=true | all-gather | bytes 557056 | tf_op jit(solution)/shard_map/all_gather | solution.py:17
  41.1 3.4 fusion.22
  44.5 2.6 psum.77
  47.1 3.8 convolution_bitcast_fusion.2
  52.3 73.3 %reduce-scatter.4.cloned.1.call-done = f32[1024,16]{0,1:T(8,128)} async-done(((f32[16384,16]{0,1:T(8,128)}), f32[1024,16]{0,1:T(8,128)}) %reduce-scatter.4.cloned.1.call-update) | async-done | bytes 65552 | tf_op jit(solution)/shard_map/reduce_scatter | solution.py:25
  127.0 50.1 %psum.78 = f32[16,384]{1,0:T(8,128)S(1)} all-reduce(f32[16,384]{1,0:T(8,128)S(1)} %fusion.23), channel_id=1, replica_groups=mesh['samp'=16,'feat'=2] {'samp','feat'}, use_global_device_ids=true, to_apply=%region_3.0 | all-reduce | flops 6144 | bytes 49152 | tf_op jit(solution)/shard_map/psum | solution.py:36
  177.8 32.0 %all_gather.10 = bf16[16,16384]{1,0:T(8,128)(2,1)S(1)} all-gather(bf16[16,1024]{1,0:T(8,128)(2,1)S(1)} %get-tuple-element.7), channel_id=1, replica_groups=mesh['samp'=16,'feat'=2] {'samp'}, dimensions={1}, use_global_device_ids=true | all-gather | bytes 557056 | tf_op jit(solution)/shard_map/all_gather | solution.py:17
  209.8 3.4 fusion.24
  213.1 2.5 psum.80
  215.6 3.8 convolution_bitcast_fusion.1
  219.5 71.6 %reduce-scatter.6.cloned.1.call-done = f32[1024,16]{0,1:T(8,128)} async-done(((f32[16384,16]{0,1:T(8,128)}), f32[1024,16]{0,1:T(8,128)}) %reduce-scatter.6.cloned.1.call-update) | async-done | bytes 65552 | tf_op jit(solution)/shard_map/reduce_scatter | solution.py:25
  292.1 2.5 psum.81
  294.6 41.5 %psum.82 = f32[16]{0:T(128)S(1)} all-reduce(f32[16]{0:T(128)S(1)} %psum.81), channel_id=1, replica_groups=mesh['samp'=16,'feat'=2] {'samp'}, use_global_device_ids=true, to_apply=%region_10.0 | all-reduce | flops 16 | bytes 128 | tf_op jit(solution)/shard_map/psum | solution.py:62
  336.0 45.4 %psum.79 = f32[16]{0:T(128)S(1)} all-reduce(f32[16]{0:T(128)S(1)} %get-tuple-element.6), channel_id=1, replica_groups=mesh['samp'=16,'feat'=2] {'samp','feat'}, use_global_device_ids=true, to_apply=%region_5.0 | all-reduce | flops 16 | bytes 128 | tf_op jit(solution)/shard_map/psum | solution.py:44
  382.8 39.4 %psum.83 = f32[16,384]{1,0:T(8,128)S(1)} all-reduce(f32[16,384]{1,0:T(8,128)S(1)} %fusion.25), channel_id=1, replica_groups=mesh['samp'=16,'feat'=2] {'samp','feat'}, use_global_device_ids=true, to_apply=%region_11.0 | all-reduce | flops 6144 | bytes 49152 | tf_op jit(solution)/shard_map/psum | solution.py:36
  423.1 40.7 %psum.84 = f32[16]{0:T(128)S(1)} all-reduce(f32[16]{0:T(128)S(1)} %get-tuple-element.9), channel_id=1, replica_groups=mesh['samp'=16,'feat'=2] {'samp','feat'}, use_global_device_ids=true, to_apply=%region_13.0 | all-reduce | flops 16 | bytes 128 | tf_op jit(solution)/shard_map/psum | solution.py:44
  463.9 31.5 %all_gather.11 = bf16[16,16384]{1,0:T(8,128)(2,1)S(1)} all-gather(bf16[16,1024]{1,0:T(8,128)(2,1)S(1)} %fusion.20), channel_id=1, replica_groups=mesh['samp'=16,'feat'=2] {'samp'}, dimensions={1}, use_global_device_ids=true | all-gather | bytes 557056 | tf_op jit(solution)/shard_map/all_gather | solution.py:17
  495.4 3.4 fusion.26
  498.8 2.5 psum.85
  501.3 3.9 convolution_bitcast_fusion
  505.2 73.3 %reduce-scatter.8.cloned.1.call-done = f32[1024,16]{0,1:T(8,128)} async-done(((f32[16384,16]{0,1:T(8,128)}), f32[1024,16]{0,1:T(8,128)}) %reduce-scatter.8.cloned.1.call-update) | async-done | bytes 65552 | tf_op jit(solution)/shard_map/reduce_scatter | solution.py:25
  578.5 1.0 fusion.1
  579.5 2.5 psum.86
  582.0 41.7 %psum.87 = f32[16]{0:T(128)S(1)} all-reduce(f32[16]{0:T(128)S(1)} %psum.86), channel_id=1, replica_groups=mesh['samp'=16,'feat'=2] {'samp'}, use_global_device_ids=true, to_apply=%region_18.0 | all-reduce | flops 16 | bytes 128 | tf_op jit(solution)/shard_map/psum | solution.py:62
  (30 shorter events, 9.1 us)
Async XLA Ops:
  6.5 120.0 %copy-start = (bf16[1024,384]{1,0:T(8,128)(2,1)S(1)}, bf16[1024,384]{1,0:T(8,128)(2,1)}, u32[]{:S(2)}) copy-start(bf16[1024,384]{1,0:T(8,128)(2,1)} %param.10) | copy-start | bytes 2359300
  6.5 119.1 %reduce-scatter.4.cloned.1.call-start = ((), (), s32[]{:S(2)}) async-start(), calls=%async_computation.3 | async-start | bytes 1114112 | tf_op jit(solution)/shard_map/reduce_scatter | solution.py:25
  44.4 6.6 %copy-start.3 = (f32[384]{0:T(512)S(1)}, f32[384]{0:T(512)}, u32[]{:S(2)}) copy-start(f32[384]{0:T(512)} %param.11) | copy-start | bytes 4612
  44.4 7.2 %copy-start.2 = (f32[16]{0:T(128)S(1)}, f32[16]{0:T(128)}, u32[]{:S(2)}) copy-start(f32[16]{0:T(128)} %param.9) | copy-start | bytes 196
  44.4 81.2 %copy-start.1 = (f32[16,1024]{1,0:T(8,128)S(1)}, f32[16,1024]{1,0:T(8,128)}, u32[]{:S(2)}) copy-start(f32[16,1024]{1,0:T(8,128)} %param.8) | copy-start | bytes 196612
  51.0 240.1 %reduce-scatter.6.cloned.1.call-start = ((), (), s32[]{:S(2)}) async-start(), calls=%async_computation.4 | async-start | bytes 1114112 | tf_op jit(solution)/shard_map/reduce_scatter | solution.py:25
  219.5 359.0 %reduce-scatter.8.cloned.1.call-start = ((), (), s32[]{:S(2)}) async-start(), calls=%async_computation.5 | async-start | bytes 1114112 | tf_op jit(solution)/shard_map/reduce_scatter | solution.py:25
Sparse Core Ops, SparseCore 0:
  51.1 74.4 reduce-scatter.3
  219.6 71.4 reduce-scatter.5
  505.3 73.1 reduce-scatter.7
